TPU v7x, 8 devices: a whole 2x2x1 slice. The times are simulated.
8 devices in a mesh: by: 4 (over z, y, x), bx: 2 (over core).
Axes of the slice: x: 2, y: 2, z: 1, core: 2. Of those that a mesh axis runs over, the one named last changes fastest.
Arguments:
- wave_fn: float32 [3072, 2, 2, 3072], P('bx', None, None, 'by')
- left_env: float32 [3072, 3, 3072], P('bx')
- mpo_ten: float32 [3, 2, 2, 3], replicated
- right_env: float32 [3072, 3, 3072], P('by')
Outputs:
- output: float32 [3072, 2, 2, 3072], P('bx', None, None, 'by')
All inputs are finite; a program needn't handle non-finite values.
Results may differ from a plain program's by a relative error of at most 0.001.
Values sent between devices are 32-bit elements.
A program may use at most 1 GiB of HBM per device.

v0:
```python
import jax
import jax.numpy as jnp
from jax import lax
from jax.sharding import PartitionSpec as P


def solution(mesh):
    prec_mode = lax.Precision.HIGHEST

    def local_apply(wave_blk, left_rows, mpo_ten, right_rows):
        row_share, mpo_dim, bond_dim = left_rows.shape
        phys_dim = wave_blk.shape[1]
        col_share = wave_blk.shape[3]
        wave_cols = lax.all_gather(wave_blk, 'bx', axis=0, tiled=True)
        stage_one = jnp.dot(left_rows.reshape(row_share * mpo_dim, bond_dim), wave_cols.reshape(bond_dim, phys_dim * phys_dim * col_share), precision=prec_mode, preferred_element_type=jnp.float32)
        stage_one = stage_one.reshape(row_share, mpo_dim, phys_dim, phys_dim, col_share)
        stage_two = jnp.einsum('aupqf,uspv->asvqf', stage_one, mpo_ten, precision=prec_mode, preferred_element_type=jnp.float32)
        stage_three = jnp.einsum('asvqf,vtqr->astrf', stage_two, mpo_ten, precision=prec_mode, preferred_element_type=jnp.float32)
        right_cols = lax.all_to_all(right_rows, 'by', 2, 0, tiled=True)
        part_sum = lax.dot_general(stage_three.reshape(row_share * phys_dim * phys_dim, mpo_dim * col_share), right_cols.reshape(bond_dim, mpo_dim * col_share), (((1,), (1,)), ((), ())), precision=prec_mode, preferred_element_type=jnp.float32)
        part_sum = part_sum.reshape(row_share, phys_dim, phys_dim, bond_dim)
        return lax.psum_scatter(part_sum, 'by', scatter_dimension=3, tiled=True)

    return jax.shard_map(local_apply, mesh=mesh, in_specs=(P('bx', None, None, 'by'), P('bx', None, None), P(), P('by', None, None)), out_specs=P('bx', None, None, 'by'), check_vma=False)
```

profile of v0, /device:TPU:0, one launch (start us, length us, event | category | flops | bytes accessed | tf_op | source)
XLA Modules:
  0.0 2819.8 jit_solution(6155563303059519737)
XLA Ops:
  6.5 0.0 copy-start
  6.5 0.0 all-gather.2.cloned.1.call-start
  6.5 0.7 all-gather.2.cloned.1.call-update
  7.3 39.0 %copy.20 = f32[768,3,3072]{0,1,2:T(4,128)} copy(f32[768,3,3072]{2,0,1:T(8,128)} %param.7) | data formatting | bytes 56623104 | tf_op args[3]
  46.3 10.5 all-to-all-start
  56.7 0.0 reduce-scatter.2.cloned.1.call-start
  56.8 0.0 copy-done
  56.8 0.6 fusion.27
  57.4 408.5 %all-to-all-done = f32[768,3,3072]{0,1,2:T(4,128)} async-done(((f32[768,3,3072]{0,1,2:T(4,128)}), f32[768,3,3072]{0,1,2:T(4,128)}, u32[]{:S(2)}, u32[]{:S(2)}) %all-to-all-start) | async-done | bytes 28311584 | tf_op jit(solution)/shard_map/all_to_all | solution.py:19
  465.9 22.8 copy.21
  488.7 25.3 copy.42
  514.0 0.0 all-gather.2.cloned.1.call-done
  514.0 54.6 %copy.34 = f32[3072,2,2,768]{0,3,2,1:T(8,128)} copy(f32[3072,2,2,768]{3,2,1,0:T(2,128)} %all-gather.2.cloned.1.call-done) | data formatting | bytes 75497472 | tf_op jit(solution)/shard_map/reshape | solution.py:15
  568.6 0.0 copy-start.2
  568.6 556.2 %fusion.12 = f32[1536,3,2,2,768,1]{4,0,3,2,1,5:T(8,128)} fusion(f32[3072,2,2,768]{0,3,2,1:T(8,128)} %copy.34, f32[1536,3,3072]{2,0,1:T(8,128)} %param.5), kind=kOutput, calls=%fused_computation.10 | convolution fusion | flops 521838526464 | bytes 150994944 | tf_op jit(solution)/shard_map/dot_general | solution.py:15
  1124.8 0.0 copy-done.2
  1124.8 265.7 %fusion.4 = f32[1536,2,768,2,3,1]{2,4,5,1,3,0:T(4,128)} fusion(f32[1536,3,2,2,768,1]{4,0,3,2,1,5:T(8,128)} %fusion.12, f32[3,2,2,3,1,1]{3,2,0,5,1,4:T(2,128)S(1)} %copy-done.2), kind=kOutput, calls=%fused_computation.4 | convolution fusion | flops 1019215872 | bytes 113246352 | tf_op jit(solution)/shard_map/aupqf,uspv->asvqf/dot_general | solution.py:17
  1390.6 144.6 %fusion.7 = f32[1536,2,2,3,768]{4,3,2,1,0:T(4,128)} fusion(f32[1536,2,768,2,3,1]{2,4,5,1,3,0:T(4,128)} %fusion.4, f32[3,2,2,3,1,1]{3,2,1,0,5,4:T(2,128)S(1)} %bitcast.58), kind=kOutput, calls=%fused_computation.7 | convolution fusion | flops 1019215872 | bytes 113246352 | tf_op jit(solution)/shard_map/asvqf,vtqr->astrf/dot_general | solution.py:18
  1535.2 76.3 %copy.19 = f32[1536,2,2,3,768]{0,4,3,2,1:T(8,128)} copy(f32[1536,2,2,3,768]{4,3,2,1,0:T(4,128)} %fusion.7) | data formatting | bytes 113246208 | tf_op jit(solution)/shard_map/asvqf,vtqr->astrf/transpose | solution.py:18
  1611.5 549.0 %fusion.10 = f32[1536,2,2,3072]{3,0,2,1:T(8,128)} fusion(f32[1536,2,2,2304]{0,3,2,1:T(8,128)} %bitcast.60, f32[3072,2304]{0,1:T(8,128)} %bitcast.61), kind=kOutput, calls=%fused_computation.8 | convolution fusion | flops 521838526464 | bytes 160432128 | tf_op jit(solution)/shard_map/dot_general | solution.py:20
  2160.5 0.0 copy-start.1
  2160.5 0.0 reduce-scatter.2.cloned.1.call-update
  2160.5 620.2 %reduce-scatter.2.cloned.1.call-done = f32[1536,2,2,768]{3,0,2,1:T(8,128)} async-done(((f32[1536,2,2,3072]{3,0,2,1:T(8,128)}), f32[1536,2,2,768]{3,0,2,1:T(8,128)}) %reduce-scatter.2.cloned.1.call-update) | async-done | bytes 18874384 | tf_op jit(solution)/shard_map/reduce_scatter | solution.py:22
  2780.7 32.0 %copy.24 = f32[1536,2,2,768]{3,2,1,0:T(2,128)} copy(f32[1536,2,2,768]{3,0,2,1:T(8,128)} %reduce-scatter.2.cloned.1.call-done) | data formatting | bytes 37748736 | tf_op jit(solution)/shard_map/reduce_scatter | solution.py:22
  2812.7 0.0 copy-done.1
Async XLA Ops:
  6.5 50.3 %copy-start = (f32[3,2,2,3]{3,2,1,0:T(2,128)S(1)}, f32[3,2,2,3]{3,2,1,0:T(2,128)}, u32[]{:S(2)}) copy-start(f32[3,2,2,3]{3,2,1,0:T(2,128)} %param.6) | copy-start | bytes 436
  6.5 507.4 %all-gather.2.cloned.1.call-start = ((), (), s32[]{:S(2)}) async-start(), calls=%async_computation.2 | async-start | bytes 56623104 | tf_op jit(solution)/shard_map/all_gather | solution.py:14
  46.3 419.6 %all-to-all-start = ((f32[768,3,3072]{0,1,2:T(4,128)}), f32[768,3,3072]{0,1,2:T(4,128)}, u32[]{:S(2)}, u32[]{:S(2)}) async-start(f32[768,3,3072]{0,1,2:T(4,128)} %copy.20), calls=%async_computation | async-start | bytes 75497472 | tf_op jit(solution)/shard_map/all_to_all | solution.py:19
  56.7 2724.0 %reduce-scatter.2.cloned.1.call-start = ((), (), s32[]{:S(2)}) async-start(), calls=%async_computation.3 | async-start | bytes 94371840 | tf_op jit(solution)/shard_map/reduce_scatter | solution.py:22
  568.6 556.2 %copy-start.2 = (f32[3,2,2,3,1,1]{3,2,0,5,1,4:T(2,128)S(1)}, f32[3,2,2,3,1,1]{3,2,0,5,1,4:T(2,128)}, u32[]{:S(2)}) copy-start(f32[3,2,2,3,1,1]{3,2,0,5,1,4:T(2,128)} %fusion.27) | copy-start | bytes 436
  2160.5 652.2 %copy-start.1 = (f32[3,2,2,3]{3,2,1,0:T(2,128)S(1)}, f32[3,2,2,3]{3,2,1,0:T(2,128)}, u32[]{:S(2)}) copy-start(f32[3,2,2,3]{3,2,1,0:T(2,128)} %param.6) | copy-start | bytes 436
Sparse Core Ops, SparseCore 0:
  8.9 57.2 all-gather.1
  2160.6 620.0 reduce-scatter.1
where the time goes:
time: 2830 us; the launch traced here: 2820 us
  matrix products  1520 us (54%)
  waiting for transfers between devices  1030 us (36%)
  local copies, waits for them, and re-layouts  251 us (9%)
    reduce_scatter x1, waiting for transfers between devices, local_apply(): return lax.psum_scatter(part_sum, 'by', scatter_dimension=3, tiled=True)  620 us
    dot_general x1, matrix products, local_apply(): jnp.dot(left_rows.reshape(row_share * mpo_dim, bond_dim), wave_cols.resha...  556 us
    dot_general x1, matrix products, local_apply(): lax.dot_general(stage_three.reshape(row_share * phys_dim * phys_dim, mpo_...  549 us
    all_to_all x1, waiting for transfers between devices, local_apply(): right_cols = lax.all_to_all(right_rows, 'by', 2, 0, tiled=True)  409 us
    dot_general x1, matrix products, local_apply(): jnp.einsum('aupqf,uspv->asvqf', stage_one, mpo_ten, precision=prec_mode,...  266 us
    dot_general x1, matrix products, local_apply(): jnp.einsum('asvqf,vtqr->astrf', stage_two, mpo_ten, precision=prec_mode,...  145 us
    transpose x1, local copies, waits for them, and re-layouts, local_apply(): jnp.einsum('asvqf,vtqr->astrf', stage_two, mpo_ten, precision=prec_mode,...  76.3 us
    unnamed x8, local copies, waits for them, and re-layouts  64.3 us
  transfers between devices with their start and end apart: 3, of which 2 were waited for; matrix products, arithmetic and copies ran while one was open for 3% of the time, Pallas kernels for 0%

commit v1 on v0

v1 whole, which is shorter than its diff:
```python
import jax
import jax.numpy as jnp
from jax import lax
from jax.experimental import pallas as pl
from jax.experimental.pallas import tpu as pltpu
from jax.sharding import PartitionSpec as P

F32 = jnp.float32
BF16 = jnp.bfloat16
LANES = 128
BLK = 256
VMEM_LIMIT = 62 * 2**20


def limbs(val):
    hi = val.astype(BF16)
    rest = val - hi.astype(F32)
    mid = rest.astype(BF16)
    return hi, mid, (rest - mid.astype(F32)).astype(BF16)


def full_product(acc, unit, lhs_limbs, rhs_limbs, transpose, reg):
    for depth, rhs in enumerate(rhs_limbs):
        pltpu.matmul_push_rhs(rhs, staging_register=reg, mxu_index=unit, transpose=transpose)
        for i in range(3 - depth):
            pltpu.matmul_acc_lhs(acc, lhs_limbs[i], load_staged_rhs=reg if i == 0 else None)
        reg = 1 - reg
    return reg


def wave_limbs(lines, k, buf, rows):
    for p in range(2):
        for q in range(2):
            for half in range(2):
                part = lines[2 * k + half, pl.ds(2 * p + q, rows, stride=4), :]
                for i, limb in enumerate(limbs(part)):
                    buf[i, p, q * rows:(q + 1) * rows, half * LANES:(half + 1) * LANES] = limb


def first_products(env_of, buf, accs, reg):
    for r in range(3):
        env = limbs(env_of(r))
        start = reg
        for p in range(2):
            reg = full_product(accs[p][r], p, [buf[i, p] for i in range(3)], env, True, start)
    return reg


def acc_refs(rows, count):
    return tuple(pltpu.ACC(unit)((rows, BLK), F32) for unit in range(2) for _ in range(count))


CT = 128
LINE_CT = 64


def to_lines_kernel(bounds, wave, *outs):
    step = pl.program_id(0)
    for out, (lo, hi) in zip(outs, bounds):
        @pl.when((step >= lo) & (step < hi))
        def _():
            for f in range(6):
                out[f] = wave[:, :, :, f * LANES:(f + 1) * LANES].reshape(LINE_CT * 4, LANES)


def from_lines_kernel(lines, out):
    for f in range(6):
        out[:, :, :, f * LANES:(f + 1) * LANES] = lines[f].reshape(LINE_CT, 2, 2, LANES)


def local_kernel(wave, right, part, lines, buf_a, buf_b, buf_c):
    bufs = (buf_a, buf_b, buf_c)

    def prepare(k):
        for f in (2 * k, 2 * k + 1):
            lines[f] = wave[:, :, :, f * LANES:(f + 1) * LANES].reshape(CT * 4, LANES)
        wave_limbs(lines, k, bufs[k], CT)

    def run(*refs):
        accs = (refs[:3], refs[3:])
        reg = 0
        prepare(0)
        for b in range(3):
            for k in range(3):
                if b == 0 and k < 2:
                    prepare(k + 1)
                reg = first_products(lambda r: right[r, b * BLK:(b + 1) * BLK, k * BLK:(k + 1) * BLK], bufs[k], accs, reg)
            for r in range(3):
                for p in range(2):
                    got = pltpu.matmul_pop(accs[p][r])
                    for q in range(2):
                        part[(p * 2 + q) * 3 + r, :, b * BLK:(b + 1) * BLK] = got[q * CT:(q + 1) * CT]

    pl.run_scoped(run, *acc_refs(2 * CT, 3))


def mix_rows(w, mid, out, row):
    rows = pl.ds(row, 8)
    for h in range(2):
        cols = slice(h * LANES, (h + 1) * LANES)
        halves = {}
        for p in range(2):
            x2 = [mid[p * 6 + i, rows, cols] for i in range(6)]
            for v in range(3):
                for t in range(2):
                    halves[v, t, p] = sum(w[v, t, q, r] * x2[q * 3 + r] for q in range(2) for r in range(3))
        for t in range(2):
            for u in range(3):
                for s in range(2):
                    out[u, s * 2 + t, rows, cols] = sum(w[u, s, p, v] * halves[v, t, p] for p in range(2) for v in range(3))


def site_tensor(w_ref):
    return {(u, s, p, v): w_ref[((u * 2 + s) * 2 + p) * 3 + v]
            for u in range(3) for s in range(2) for p in range(2) for v in range(3)}


def remote_kernel(n_tiles, own_ref, w_ref, wave, right, part, out, buf_a, buf_b, buf_c, mid):
    bufs = (buf_a, buf_b, buf_c)
    step = pl.program_id(0)
    own = own_ref[0]
    w = site_tensor(w_ref)
    groups = CT // 8

    def run(*refs):
        accs = (refs[:3], refs[3:])

        @pl.when(step < n_tiles)
        def _():
            wave_limbs(wave.at[lax.rem(own + 1, 4)], 0, bufs[0], CT)

            def shard_step(m, carry):
                shard = lax.rem(own + 1 + m, 4)
                later = lax.rem(own + 1 + jnp.minimum(m + 1, 2), 4)
                reg = 0
                for k in range(3):
                    if k < 2:
                        wave_limbs(wave.at[shard], k + 1, bufs[k + 1], CT)
                    else:
                        wave_limbs(wave.at[later], 0, bufs[0], CT)
                    for g in range(2):
                        row = jnp.minimum(m * 6 + k * 2 + g, groups - 1) * 8
                        mix_rows(w, mid, out, pl.multiple_of(row, 8))
                    first = pl.multiple_of(shard * 768 + k * BLK, BLK)
                    reg = first_products(lambda r: right[r, :, pl.ds(first, BLK)], bufs[k], accs, reg)
                return carry

            lax.fori_loop(0, 3, shard_step, 0)
            for r in range(3):
                for p in range(2):
                    got = pltpu.matmul_pop(accs[p][r])
                    for q in range(2):
                        i = (p * 2 + q) * 3 + r
                        mid[i] = got[q * CT:(q + 1) * CT] + part[i]

        @pl.when(step == n_tiles)
        def _():
            def group(g, carry):
                mix_rows(w, mid, out, pl.multiple_of(g * 8, 8))
                return carry

            lax.fori_loop(0, groups, group, 0)

    pl.run_scoped(run, *acc_refs(2 * CT, 3))


AT = 768


def second_kernel(n_src, has_prev, final, *refs):
    lefts, zs, refs = refs[:n_src], refs[n_src:2 * n_src], refs[2 * n_src:]
    prev, refs = (refs[0], refs[1:]) if has_prev else (None, refs)
    out, buf_a, buf_b = refs
    bufs = (buf_a, buf_b)
    col = pl.program_id(1)

    def run(acc0, acc1):
        steps = [(m, u) for m in range(n_src) for u in range(3)]

        def left_limbs(n):
            m, u = steps[n]
            for i, limb in enumerate(limbs(lefts[m][u])):
                bufs[n % 2][i] = limb

        left_limbs(0)
        reg = 0
        for n, (m, u) in enumerate(steps):
            if n + 1 < len(steps):
                left_limbs(n + 1)
            start = reg
            for t, acc in enumerate((acc0, acc1)):
                reg = full_product(acc, t, [bufs[n % 2][i] for i in range(3)], limbs(zs[m][u, t]), False, start)
        for t, acc in enumerate((acc0, acc1)):
            got = pltpu.matmul_pop(acc)
            if has_prev:
                got = got + prev[:, t * BLK:(t + 1) * BLK]
            if final:
                for half in range(2):
                    out[half, pl.ds(2 * (col % 2) + t, AT, stride=4), :] = got[:, half * LANES:(half + 1) * LANES]
            else:
                out[:, t * BLK:(t + 1) * BLK] = got

    pl.run_scoped(run, pltpu.ACC(0)((AT, BLK), F32), pltpu.ACC(1)((AT, BLK), F32))


def params():
    return pltpu.CompilerParams(vmem_limit_bytes=VMEM_LIMIT)


def cost(flops, nbytes):
    return pl.CostEstimate(flops=flops, bytes_accessed=nbytes, transcendentals=0)


def solution(mesh):
    def local_apply(wave_blk, left_rows, mpo_ten, right_rows):
        rows_c, cols_f = wave_blk.shape[0], wave_blk.shape[3]
        n_by = 4
        chunk = 256
        n_chunk = rows_c // chunk
        tiles = chunk // CT
        by, bx = lax.axis_index('by'), lax.axis_index('bx')
        left = left_rows.transpose(1, 0, 2)
        right = right_rows.transpose(1, 0, 2)
        mpo_flat = mpo_ten.reshape(-1)
        own = by.astype(jnp.int32)[None]
        line_steps = chunk // LINE_CT

        def to_lines(lo, hi):
            n = hi - lo
            bounds = [(j * line_steps, (j + 1) * line_steps) for j in range(n)]
            return pl.pallas_call(
                lambda *refs: to_lines_kernel(bounds, *refs),
                grid=(n * line_steps,),
                in_specs=[pl.BlockSpec((LINE_CT, 2, 2, cols_f), lambda i: (lo * line_steps + i, 0, 0, 0))],
                out_specs=[pl.BlockSpec((6, LINE_CT * 4, LANES), lambda i, j=j: (0, jnp.clip(i - j * line_steps, 0, line_steps - 1), 0)) for j in range(n)],
                out_shape=[jax.ShapeDtypeStruct((6, chunk * 4, LANES), F32)] * n,
                compiler_params=params(),
                cost_estimate=cost(10**9 * n, 8 * n * 2**20),
                name='to_lines',
            )(wave_blk)

        lines = to_lines(0, 1) + to_lines(1, n_chunk)
        gathered = [lax.all_gather(line, 'by', axis=0, tiled=False) for line in lines]

        part = pl.pallas_call(
            lambda idx, *refs: local_kernel(*refs),
            grid_spec=pltpu.PrefetchScalarGridSpec(
                num_scalar_prefetch=1,
                grid=(rows_c // CT,),
                in_specs=[
                    pl.BlockSpec((CT, 2, 2, cols_f), lambda i, idx: (i, 0, 0, 0)),
                    pl.BlockSpec((3, 768, 768), lambda i, idx: (0, 0, idx[0]), pipeline_mode=pl.Buffered(1)),
                ],
                out_specs=pl.BlockSpec((12, CT, 768), lambda i, idx: (0, i, 0)),
                scratch_shapes=[pltpu.VMEM((6, CT * 4, LANES), F32)] + [pltpu.VMEM((3, 2, 2 * CT, BLK), BF16)] * 3,
            ),
            out_shape=jax.ShapeDtypeStruct((12, rows_c, 768), F32),
            compiler_params=params(),
            cost_estimate=cost(2 * rows_c * 4 * 768 * 2304 * 6, 120 * 2**20),
            name='local_part',
        )(own, wave_blk, right)

        def first(k, got):
            n_tiles = tiles * 3

            def tile(i):
                return jnp.minimum(i, n_tiles - 1)

            def done(i):
                return jnp.maximum(i - 1, 0)

            return pl.pallas_call(
                lambda *refs: remote_kernel(n_tiles, *refs),
                grid_spec=pltpu.PrefetchScalarGridSpec(
                    num_scalar_prefetch=1,
                    grid=(n_tiles + 1,),
                    in_specs=[
                        pl.BlockSpec(memory_space=pltpu.SMEM),
                        pl.BlockSpec((4, 6, CT * 4, LANES), lambda i, idx: (0, 0, tile(i) % tiles, 0)),
                        pl.BlockSpec((3, BLK, 3072), lambda i, idx: (0, tile(i) // tiles, 0)),
                        pl.BlockSpec((12, CT, BLK), lambda i, idx: (0, k * tiles + tile(i) % tiles, tile(i) // tiles)),
                    ],
                    out_specs=pl.BlockSpec((3, 4, CT, BLK), lambda i, idx: (0, 0, done(i) % tiles, done(i) // tiles)),
                    scratch_shapes=[pltpu.VMEM((3, 2, 2 * CT, BLK), BF16)] * 3 + [pltpu.VMEM((12, CT, BLK), F32)],
                ),
                out_shape=jax.ShapeDtypeStruct((3, 4, chunk, 768), F32),
                compiler_params=params(),
                cost_estimate=cost(2 * chunk * 4 * 2304 * 2304 * 6, 60 * 2**20),
                name='remote_part',
            )(own, mpo_flat, got, right, part)

        def second(group, mine, theirs, prev, final):
            srcs = [(bx, k) for k in group] + [(1 - bx, k) for k in group]
            where = jnp.stack([b * n_chunk + k for b, k in srcs]).astype(jnp.int32)
            n_src = len(srcs)
            in_specs = [pl.BlockSpec((3, AT, chunk), lambda a, n, idx, m=m: (0, a, idx[m])) for m in range(n_src)]
            in_specs += [pl.BlockSpec((3, 2, chunk, BLK), lambda a, n, idx: (0, n % 2, 0, n // 2))] * n_src
            operands = [left] * n_src + mine + theirs
            if prev is not None:
                in_specs.append(pl.BlockSpec((AT, 2 * BLK), lambda a, n, idx: (a, n)))
                operands.append(prev)
            if final:
                out_spec = pl.BlockSpec((2, AT * 4, LANES), lambda a, n, idx: (n // 2, a, 0))
                out_shape = jax.ShapeDtypeStruct((6, rows_c * 4, LANES), F32)
            else:
                out_spec = pl.BlockSpec((AT, 2 * BLK), lambda a, n, idx: (a, n))
                out_shape = jax.ShapeDtypeStruct((rows_c, 3072), F32)
            return pl.pallas_call(
                lambda idx, *refs: second_kernel(n_src, prev is not None, final, *refs),
                grid_spec=pltpu.PrefetchScalarGridSpec(
                    num_scalar_prefetch=1,
                    grid=(rows_c // AT, 6),
                    in_specs=in_specs,
                    out_specs=out_spec,
                    scratch_shapes=[pltpu.VMEM((3, AT, BLK), BF16)] * 2,
                ),
                out_shape=out_shape,
                compiler_params=params(),
                cost_estimate=cost(2 * rows_c * 3072 * 3 * chunk * n_src * 6, 100 * 2**20),
                name='second_part',
            )(where, *operands)

        mine, theirs = [], []

        def stage(k):
            z = first(k, gathered[k])
            mine.append(z)
            theirs.append(lax.ppermute(z, 'bx', [(0, 1), (1, 0)]))

        def apply(group, prev, final):
            return second(group, [mine[k] for k in group], [theirs[k] for k in group], prev, final)

        def after(k, val):
            gathered[k], val = lax.optimization_barrier((gathered[k], val))
            return val

        stage(0)
        stage(1)
        acc = apply([0], None, False)
        acc = after(2, acc)
        stage(2)
        stage(3)
        acc = apply([1, 2], acc, False)
        acc = after(4, acc)
        stage(4)
        stage(5)
        acc = apply([3, 4], acc, False)
        acc = apply([5], acc, True)
        return pl.pallas_call(
            from_lines_kernel,
            grid=(rows_c // LINE_CT,),
            in_specs=[pl.BlockSpec((6, LINE_CT * 4, LANES), lambda i: (0, i, 0))],
            out_specs=pl.BlockSpec((LINE_CT, 2, 2, cols_f), lambda i: (i, 0, 0, 0)),
            out_shape=jax.ShapeDtypeStruct((rows_c, 2, 2, cols_f), F32),
            compiler_params=params(),
            name='from_lines',
        )(acc)

    return jax.shard_map(local_apply, mesh=mesh, in_specs=(P('bx', None, None, 'by'), P('bx', None, None), P(), P('by', None, None)), out_specs=P('bx', None, None, 'by'), check_vma=False)
```

time: 2830 us -> 1330 us (0.47)
  matrix products: 1520 us -> 0 us
  Pallas kernels: 0 us -> 1300 us
  waiting for transfers between devices: 1030 us -> 1.29 us
  local copies, waits for them, and re-layouts: 251 us -> 0.67 us
    dot_general x4 -> x0, matrix products: 1520 us -> none  [the longest x1 556 us: local_apply(): jnp.dot(left_rows.reshape(row_share * mpo_dim, bond_dim), wave_cols.resha...]
    pallas_call x0 -> x14, Pallas kernels: none -> 1300 us  [the longest x4 571 us: second(): pl.pallas_call(lambda idx, *refs: second_kernel(n_src, prev is not None,...]
    reduce_scatter x1 -> x0, waiting for transfers between devices: 620 us -> none  [local_apply(): return lax.psum_scatter(part_sum, 'by', scatter_dimension=3, tiled=True)]
    all_to_all x1 -> x0, waiting for transfers between devices: 409 us -> none  [local_apply(): right_cols = lax.all_to_all(right_rows, 'by', 2, 0, tiled=True)]
    transpose x1 -> x0, local copies, waits for them, and re-layouts: 76.3 us -> none  [local_apply(): jnp.einsum('asvqf,vtqr->astrf', stage_two, mpo_ten, precision=prec_mode,...]
    unnamed x8 -> x2, local copies, waits for them, and re-layouts: 64.3 us -> 0.01 us
    reshape x1, local copies, waits for them, and re-layouts: 54.6 us -> 0.67 us  [local_apply(): mpo_flat = mpo_ten.reshape(-1)]
    reduce_scatter x1 -> x0, local copies, waits for them, and re-layouts: 32 us -> none  [local_apply(): return lax.psum_scatter(part_sum, 'by', scatter_dimension=3, tiled=True)]
  transfers between devices with their start and end apart: 3 -> 12, of which waited for: 2 -> 0; matrix products, arithmetic and copies ran while one was open for 3% -> 0% of each run, Pallas kernels for 0% -> 89%
where the time goes in v1:
time: 1330 us; the launch traced here: 1320 us
  Pallas kernels  1300 us (98%)
  between operations  13.8 us (1%)
    pallas_call x4, Pallas kernels, second(): pl.pallas_call(lambda idx, *refs: second_kernel(n_src, prev is not None,...  571 us
    pallas_call x6, Pallas kernels, first(): pl.pallas_call(lambda *refs: remote_kernel(n_tiles, *refs), grid_spec=plt...  535 us
    pallas_call x1, Pallas kernels, local_apply(): pl.pallas_call(lambda idx, *refs: local_kernel(*refs), grid_spec=pltpu.Pr...  145 us
  transfers between devices with their start and end apart: 12, of which 0 were waited for; matrix products, arithmetic and copies ran while one was open for 0% of the time, Pallas kernels for 89%

profile of v1, /device:TPU:0, one launch (start us, length us, event | category | flops | bytes accessed | tf_op | source)
XLA Modules:
  0.0 1318.6 jit_solution(11924597782937511124)
XLA Ops:
  6.5 4.5 to_lines.3
  11.0 0.0 all-gather.23.cloned.1.call-update
  11.0 0.0 all-gather.19.cloned.1.call-start
  11.1 19.1 %to_lines.2 = (f32[6,1024,128]{2,1,0:T(8,128)}, f32[6,1024,128]{2,1,0:T(8,128)}, f32[6,1024,128]{2,1,0:T(8,128)}, f32[6,1024,128]{2,1,0:T(8,128)}, f32[6,1024,128]{2,1,0:T(8,128)}) custom-call(f32[1536,2,2,768]{3,2,1,0:T(2,128)} %refs_0_.5), custom_call_target="tpu_custom_call" | custom-call | flops 5000000000 | bytes 41943040 | tf_op jit(solution)/shard_map/to_lines/pallas_call | solution.py:231
  30.2 0.0 all-gather.19.cloned.1.call-update
  30.2 0.0 all-gather.21.cloned.1.call-start
  30.3 0.7 all-gather.21.cloned.1.call-update
  31.0 0.0 all-gather.15.cloned.1.call-start
  31.0 0.5 all-gather.15.cloned.1.call-update
  31.5 0.0 all-gather.17.cloned.1.call-start
  31.6 0.7 reshape.3.refs_1_
  32.3 144.7 %local_part.1.refs_4_ = f32[12,1536,768]{2,1,0:T(8,128)} custom-call(s32[1]{0:T(128)} %bitcast.3.idx.refs_0_, f32[1536,2,2,768]{3,2,1,0:T(2,128)} %refs_0_.5, f32[3,768,3072]{2,1,0:T(8,128)} %bitcast.33), custom_call_target="tpu_custom_call" | custom-call | flops 130459631616 | bytes 125829120 | tf_op jit(solution)/shard_map/local_part/pallas_call | solution.py:245
  177.0 89.3 %remote_part.9.refs_2_ = f32[3,4,256,768]{3,2,1,0:T(8,128)} custom-call(s32[1]{0:T(128)} %bitcast.3.idx.refs_0_, f32[36]{0:T(128)} %reshape.3.refs_1_, f32[4,6,1024,128]{3,2,1,0:T(8,128)} %bitcast.45, f32[3,768,3072]{2,1,0:T(8,128)} %bitcast.34, f32[12,1536,768]{2,1,0:T(8,128)} %local_part.1.refs_4_), custom_call_target="tpu_custom_call" | custom-call | flops 65229815808 | bytes 62914560 | tf_op jit(solution)/shard_map/remote_part/pallas_call | solution.py:272
  266.3 0.8 collective-permute-start.1
  267.1 0.0 all-gather.13.cloned.1.call-start
  267.2 0.6 pad_add_fusion.3.idx
  267.8 89.0 %remote_part.8.refs_4_ = f32[3,4,256,768]{3,2,1,0:T(8,128)} custom-call(s32[1]{0:T(128)} %bitcast.3.idx.refs_0_, f32[36]{0:T(128)} %reshape.3.refs_1_, f32[4,6,1024,128]{3,2,1,0:T(8,128)} %bitcast.44, f32[3,768,3072]{2,1,0:T(8,128)} %bitcast.35, f32[12,1536,768]{2,1,0:T(8,128)} %local_part.1.refs_4_), custom_call_target="tpu_custom_call" | custom-call | flops 65229815808 | bytes 62914560 | tf_op jit(solution)/shard_map/remote_part/pallas_call | solution.py:272
  356.8 96.3 %second_part.4.refs_8_ = f32[1536,3072]{1,0:T(8,128)} custom-call(s32[2]{0:T(128)} %pad_add_fusion.3.idx, f32[3,1536,3072]{2,1,0:T(8,128)} %bitcast.21, f32[3,1536,3072]{2,1,0:T(8,128)} %bitcast.22, f32[3,4,256,768]{3,2,1,0:T(8,128)} %remote_part.9.refs_2_, f32[3,4,256,768]{3,2,1,0:T(8,128)} %collective-permute-done.1.refs_3_), custom_call_target="tpu_custom_call" | custom-call | flops 86973087744 | bytes 104857600 | tf_op jit(solution)/shard_map/second_part/pallas_call | solution.py:308
  453.1 89.3 %remote_part.10.refs_5_ = f32[3,4,256,768]{3,2,1,0:T(8,128)} custom-call(s32[1]{0:T(128)} %bitcast.3.idx.refs_0_, f32[36]{0:T(128)} %reshape.3.refs_1_, f32[4,6,1024,128]{3,2,1,0:T(8,128)} %bitcast.42, f32[3,768,3072]{2,1,0:T(8,128)} %bitcast.36, f32[12,1536,768]{2,1,0:T(8,128)} %local_part.1.refs_4_), custom_call_target="tpu_custom_call" | custom-call | flops 65229815808 | bytes 62914560 | tf_op jit(solution)/shard_map/remote_part/pallas_call | solution.py:272
  542.4 0.5 collective-permute-start.3
  542.9 0.6 pad_add_fusion.2.idx
  543.5 89.1 %remote_part.7.refs_4_ = f32[3,4,256,768]{3,2,1,0:T(8,128)} custom-call(s32[1]{0:T(128)} %bitcast.3.idx.refs_0_, f32[36]{0:T(128)} %reshape.3.refs_1_, f32[4,6,1024,128]{3,2,1,0:T(8,128)} %bitcast.40, f32[3,768,3072]{2,1,0:T(8,128)} %bitcast.37, f32[12,1536,768]{2,1,0:T(8,128)} %local_part.1.refs_4_), custom_call_target="tpu_custom_call" | custom-call | flops 65229815808 | bytes 62914560 | tf_op jit(solution)/shard_map/remote_part/pallas_call | solution.py:272
  632.6 188.5 %second_part.5.refs_8_ = f32[1536,3072]{1,0:T(8,128)} custom-call(s32[4]{0:T(128)} %pad_add_fusion.2.idx, f32[3,1536,3072]{2,1,0:T(8,128)} %bitcast.23, f32[3,1536,3072]{2,1,0:T(8,128)} %bitcast.24, f32[3,1536,3072]{2,1,0:T(8,128)} %bitcast.25, f32[3,1536,3072]{2,1,0:T(8,128)} %bitcast.26, f32[3,4,256,768]{3,2,1,0:T(8,128)} %remote_part.8.refs_4_, ...), custom_call_target="tpu_custom_call" | custom-call | flops 173946175488 | bytes 104857600 | tf_op jit(solution)/shard_map/second_part/pallas_call | solution.py:308
  821.1 89.2 %remote_part.11.refs_5_ = f32[3,4,256,768]{3,2,1,0:T(8,128)} custom-call(s32[1]{0:T(128)} %bitcast.3.idx.refs_0_, f32[36]{0:T(128)} %reshape.3.refs_1_, f32[4,6,1024,128]{3,2,1,0:T(8,128)} %bitcast.41, f32[3,768,3072]{2,1,0:T(8,128)} %bitcast.38, f32[12,1536,768]{2,1,0:T(8,128)} %local_part.1.refs_4_), custom_call_target="tpu_custom_call" | custom-call | flops 65229815808 | bytes 62914560 | tf_op jit(solution)/shard_map/remote_part/pallas_call | solution.py:272
  910.3 0.5 collective-permute-start.5
  910.8 0.6 pad_add_fusion.idx
  911.4 0.6 pad_add_fusion.1.idx
  912.0 89.0 %remote_part.6.refs_2_ = f32[3,4,256,768]{3,2,1,0:T(8,128)} custom-call(s32[1]{0:T(128)} %bitcast.3.idx.refs_0_, f32[36]{0:T(128)} %reshape.3.refs_1_, f32[4,6,1024,128]{3,2,1,0:T(8,128)} %bitcast.43, f32[3,768,3072]{2,1,0:T(8,128)} %bitcast.39, f32[12,1536,768]{2,1,0:T(8,128)} %local_part.1.refs_4_), custom_call_target="tpu_custom_call" | custom-call | flops 65229815808 | bytes 62914560 | tf_op jit(solution)/shard_map/remote_part/pallas_call | solution.py:272
  1001.1 0.0 collective-permute-start
  1001.1 188.2 %second_part.6.refs_4_ = f32[1536,3072]{1,0:T(8,128)} custom-call(s32[4]{0:T(128)} %pad_add_fusion.1.idx, f32[3,1536,3072]{2,1,0:T(8,128)} %bitcast.27, f32[3,1536,3072]{2,1,0:T(8,128)} %bitcast.28, f32[3,1536,3072]{2,1,0:T(8,128)} %bitcast.29, f32[3,1536,3072]{2,1,0:T(8,128)} %bitcast.30, f32[3,4,256,768]{3,2,1,0:T(8,128)} %remote_part.7.refs_4_, ...), custom_call_target="tpu_custom_call" | custom-call | flops 173946175488 | bytes 104857600 | tf_op jit(solution)/shard_map/second_part/pallas_call | solution.py:308
  1189.3 97.8 %second_part.7.lines = f32[6,6144,128]{2,1,0:T(8,128)} custom-call(s32[2]{0:T(128)} %pad_add_fusion.idx, f32[3,1536,3072]{2,1,0:T(8,128)} %bitcast.31, f32[3,1536,3072]{2,1,0:T(8,128)} %bitcast.32, f32[3,4,256,768]{3,2,1,0:T(8,128)} %remote_part.6.refs_2_, f32[3,4,256,768]{3,2,1,0:T(8,128)} %collective-permute-done.refs_3_, f32[1536,3072]{1,0:T(8,128)} %second_part.6.refs_4_), custom_call_target="tpu_custom_call" | custom-call | flops 86973087744 | bytes 104857600 | tf_op jit(solution)/shard_map/second_part/pallas_call | solution.py:308
  1287.1 24.4 %from_lines.1 = f32[1536,2,2,768]{3,2,1,0:T(2,128)} custom-call(f32[6,6144,128]{2,1,0:T(8,128)} %second_part.7.lines), custom_call_target="tpu_custom_call" | custom-call | tf_op jit(solution)/shard_map/from_lines/pallas_call | solution.py:349
  (19 shorter events, 0.1 us)
Async XLA Ops:
  6.5 170.5 %all-gather.23.cloned.1.call-start = ((), (), s32[]{:S(2)}) async-start(), calls=%async_computation.5 | async-start | bytes 15728640 | tf_op jit(solution)/shard_map/all_gather | solution.py:243
  11.0 256.8 %all-gather.19.cloned.1.call-start = ((), (), s32[]{:S(2)}) async-start(), calls=%async_computation.3 | async-start | bytes 15728640 | tf_op jit(solution)/shard_map/all_gather | solution.py:243
  30.2 1.4 copy-start
  30.2 422.9 %all-gather.21.cloned.1.call-start = ((), (), s32[]{:S(2)}) async-start(), calls=%async_computation.4 | async-start | bytes 15728640 | tf_op jit(solution)/shard_map/all_gather | solution.py:243
  31.0 512.5 %all-gather.15.cloned.1.call-start = ((), (), s32[]{:S(2)}) async-start(), calls=%async_computation.1 | async-start | bytes 15728640 | tf_op jit(solution)/shard_map/all_gather | solution.py:243
  31.5 789.6 %all-gather.17.cloned.1.call-start = ((), (), s32[]{:S(2)}) async-start(), calls=%async_computation.2 | async-start | bytes 15728640 | tf_op jit(solution)/shard_map/all_gather | solution.py:243
  266.3 90.6 %collective-permute-start.1 = (f32[3,4,256,768]{3,2,1,0:T(8,128)}, f32[3,4,256,768]{3,2,1,0:T(8,128)}, u32[]{:S(2)}, u32[]{:S(2)}) collective-permute-start(f32[3,4,256,768]{3,2,1,0:T(8,128)} %remote_part.9.refs_2_), channel_id=1, source_target_pairs={{0,1},{1,0},{2,3},{3,2},{4,5},{5,4},{6,7},{7,6}} | collective-permute-start | bytes 28311560 | tf_op jit(solution)/shard_map/ppermute | solution.py:328
  267.1 644.9 %all-gather.13.cloned.1.call-start = ((), (), s32[]{:S(2)}) async-start(), calls=%async_computation | async-start | bytes 15728640 | tf_op jit(solution)/shard_map/all_gather | solution.py:243
  356.8 275.8 %collective-permute-start.2 = (f32[3,4,256,768]{3,2,1,0:T(8,128)}, f32[3,4,256,768]{3,2,1,0:T(8,128)}, u32[]{:S(2)}, u32[]{:S(2)}) collective-permute-start(f32[3,4,256,768]{3,2,1,0:T(8,128)} %remote_part.8.refs_4_), channel_id=1, source_target_pairs={{0,1},{1,0},{2,3},{3,2},{4,5},{5,4},{6,7},{7,6}} | collective-permute-start | bytes 28311560 | tf_op jit(solution)/shard_map/ppermute | solution.py:328
  542.4 90.2 %collective-permute-start.3 = (f32[3,4,256,768]{3,2,1,0:T(8,128)}, f32[3,4,256,768]{3,2,1,0:T(8,128)}, u32[]{:S(2)}, u32[]{:S(2)}) collective-permute-start(f32[3,4,256,768]{3,2,1,0:T(8,128)} %remote_part.10.refs_5_), channel_id=1, source_target_pairs={{0,1},{1,0},{2,3},{3,2},{4,5},{5,4},{6,7},{7,6}} | collective-permute-start | bytes 28311560 | tf_op jit(solution)/shard_map/ppermute | solution.py:328
  632.6 368.5 %collective-permute-start.4 = (f32[3,4,256,768]{3,2,1,0:T(8,128)}, f32[3,4,256,768]{3,2,1,0:T(8,128)}, u32[]{:S(2)}, u32[]{:S(2)}) collective-permute-start(f32[3,4,256,768]{3,2,1,0:T(8,128)} %remote_part.7.refs_4_), channel_id=1, source_target_pairs={{0,1},{1,0},{2,3},{3,2},{4,5},{5,4},{6,7},{7,6}} | collective-permute-start | bytes 28311560 | tf_op jit(solution)/shard_map/ppermute | solution.py:328
  910.3 90.8 %collective-permute-start.5 = (f32[3,4,256,768]{3,2,1,0:T(8,128)}, f32[3,4,256,768]{3,2,1,0:T(8,128)}, u32[]{:S(2)}, u32[]{:S(2)}) collective-permute-start(f32[3,4,256,768]{3,2,1,0:T(8,128)} %remote_part.11.refs_5_), channel_id=1, source_target_pairs={{0,1},{1,0},{2,3},{3,2},{4,5},{5,4},{6,7},{7,6}} | collective-permute-start | bytes 28311560 | tf_op jit(solution)/shard_map/ppermute | solution.py:328
  1001.1 188.3 %collective-permute-start = (f32[3,4,256,768]{3,2,1,0:T(8,128)}, f32[3,4,256,768]{3,2,1,0:T(8,128)}, u32[]{:S(2)}, u32[]{:S(2)}) collective-permute-start(f32[3,4,256,768]{3,2,1,0:T(8,128)} %remote_part.6.refs_2_), channel_id=1, source_target_pairs={{0,1},{1,0},{2,3},{3,2},{4,5},{5,4},{6,7},{7,6}} | collective-permute-start | bytes 28311560 | tf_op jit(solution)/shard_map/ppermute | solution.py:328
Sparse Core Ops, SparseCore 0:
  11.1 119.6 all-gather.22
  132.6 116.8 all-gather.18
  251.3 116.8 all-gather.20
  369.8 116.8 all-gather.14
  488.3 116.8 all-gather.16
  606.7 116.8 all-gather.12

commit v2 on v1

v2 whole, which is shorter than its diff:
```python
import jax
import jax.numpy as jnp
from jax import lax
from jax.experimental import pallas as pl
from jax.experimental.pallas import tpu as pltpu
from jax.sharding import PartitionSpec as P

F32 = jnp.float32
BF16 = jnp.bfloat16
LANES = 128
BLK = 256
VMEM_LIMIT = 62 * 2**20


def limbs(val):
    hi = val.astype(BF16)
    rest = val - hi.astype(F32)
    mid = rest.astype(BF16)
    return hi, mid, (rest - mid.astype(F32)).astype(BF16)


def full_product(acc, unit, lhs_limbs, rhs_limbs, transpose, reg):
    for depth, rhs in enumerate(rhs_limbs):
        pltpu.matmul_push_rhs(rhs, staging_register=reg, mxu_index=unit, transpose=transpose)
        for i in range(3 - depth):
            pltpu.matmul_acc_lhs(acc, lhs_limbs[i], load_staged_rhs=reg if i == 0 else None)
        reg = 1 - reg
    return reg


PIECE = 64


def wave_limbs(lines, k, buf, rows):
    for p in range(2):
        for q in range(2):
            for top in range(0, rows, PIECE):
                for half in range(2):
                    part = lines[2 * k + half, pl.ds(4 * top + 2 * p + q, PIECE, stride=4), :]
                    for i, limb in enumerate(limbs(part)):
                        buf[i, p, q * rows + top:q * rows + top + PIECE, half * LANES:(half + 1) * LANES] = limb


def first_products(env_of, buf, accs, reg):
    for r in range(3):
        env = limbs(env_of(r))
        start = reg
        for p in range(2):
            reg = full_product(accs[p][r], p, [buf[i, p] for i in range(3)], env, True, start)
    return reg


def acc_refs(rows, count):
    return tuple(pltpu.ACC(unit)((rows, BLK), F32) for unit in range(2) for _ in range(count))


CT = 128
LINE_CT = 128


def line_copies(wave, first, rows, lines, sems):
    return [
        pltpu.make_async_copy(
            wave.at[pl.ds(first, rows), :, :, pl.ds(f * LANES, LANES)], lines.at[f].reshape(rows, 2, 2, LANES), sems.at[f])
        for f in range(6)
    ]


def to_lines_kernel(base, bounds, wave, *refs):
    outs, sems = refs[:-1], refs[-1]
    step = pl.program_id(0)
    for out, (lo, hi) in zip(outs, bounds):
        @pl.when((step >= lo) & (step < hi))
        def _():
            copies = line_copies(wave, base + step * LINE_CT, LINE_CT, out, sems)
            for copy in copies:
                copy.start()
            for copy in copies:
                copy.wait()


def local_kernel(n_tiles, wave, right, part, lines, sems, buf_a, buf_b, buf_c):
    bufs = (buf_a, buf_b, buf_c)
    step = pl.program_id(0)
    slot = lax.rem(step, 2)

    def copies(tile, at):
        return line_copies(wave, tile * CT, CT, lines.at[at], sems.at[at])

    @pl.when(step == 0)
    def _():
        for copy in copies(0, 0):
            copy.start()

    @pl.when(step + 1 < n_tiles)
    def _():
        for copy in copies(step + 1, 1 - slot):
            copy.start()

    for copy in copies(step, slot):
        copy.wait()
    here = lines.at[slot]

    def run(*refs):
        accs = (refs[:3], refs[3:])
        reg = 0
        wave_limbs(here, 0, bufs[0], CT)
        for b in range(3):
            for k in range(3):
                if b == 0 and k < 2:
                    wave_limbs(here, k + 1, bufs[k + 1], CT)
                reg = first_products(lambda r: right[r, b * BLK:(b + 1) * BLK, k * BLK:(k + 1) * BLK], bufs[k], accs, reg)
            for r in range(3):
                for p in range(2):
                    got = pltpu.matmul_pop(accs[p][r])
                    for q in range(2):
                        part[(p * 2 + q) * 3 + r, :, b * BLK:(b + 1) * BLK] = got[q * CT:(q + 1) * CT]

    pl.run_scoped(run, *acc_refs(2 * CT, 3))


def mix_rows(w, mid, out, row):
    rows = pl.ds(row, 8)
    for h in range(2):
        cols = slice(h * LANES, (h + 1) * LANES)
        halves = {}
        for p in range(2):
            x2 = [mid[p * 6 + i, rows, cols] for i in range(6)]
            for v in range(3):
                for t in range(2):
                    halves[v, t, p] = sum(w[v, t, q, r] * x2[q * 3 + r] for q in range(2) for r in range(3))
        for t in range(2):
            for u in range(3):
                for s in range(2):
                    out[u, s * 2 + t, rows, cols] = sum(w[u, s, p, v] * halves[v, t, p] for p in range(2) for v in range(3))


def site_tensor(w_ref):
    return {(u, s, p, v): w_ref[((u * 2 + s) * 2 + p) * 3 + v]
            for u in range(3) for s in range(2) for p in range(2) for v in range(3)}


def remote_kernel(own_ref, w_ref, wave, right, part, out, wave_buf, mid):
    own = own_ref[0]
    w = site_tensor(w_ref)

    def run(*refs):
        accs = (refs[:3], refs[3:])

        @pl.when(pl.program_id(0) % 3 == 0)
        def _():
            def split(m, carry):
                for k in range(3):
                    wave_limbs(wave.at[lax.rem(own + 1 + m, 4)], k, wave_buf.at[3 * m + k], CT)
                return carry

            lax.fori_loop(0, 3, split, 0)

        def shard_step(m, carry):
            shard = lax.rem(own + 1 + m, 4)
            reg = 0
            for k in range(3):
                first = pl.multiple_of(shard * 768 + k * BLK, BLK)
                buf = wave_buf.at[3 * m + k]
                reg = first_products(lambda r: right[r, :, pl.ds(first, BLK)], buf, accs, reg)
            return carry

        lax.fori_loop(0, 3, shard_step, 0)
        for r in range(3):
            for p in range(2):
                got = pltpu.matmul_pop(accs[p][r])
                for q in range(2):
                    i = (p * 2 + q) * 3 + r
                    mid[i] = got[q * CT:(q + 1) * CT] + part[i]

        def mix_step(g, carry):
            mix_rows(w, mid, out, pl.multiple_of(g * 8, 8))
            return carry

        lax.fori_loop(0, CT // 8, mix_step, 0)

    pl.run_scoped(run, *acc_refs(2 * CT, 3))


AT = 768


def second_kernel(n_src, width, has_prev, final, *refs):
    lefts, zs, refs = refs[:n_src], refs[n_src:2 * n_src], refs[2 * n_src:]
    prev, refs = (refs[0], refs[1:]) if has_prev else (None, refs)
    out, buf_a, buf_b, zbuf_a, zbuf_b = refs[:5]
    bufs, zbufs = (buf_a, buf_b), (zbuf_a, zbuf_b)
    row, col = pl.program_id(0), pl.program_id(1)
    steps = [(m, u, j * BLK) for m in range(n_src) for u in range(3) for j in range(width // BLK)]

    if final:
        lines, sems = refs[5:]
        turn = row * 3 + col // 2
        slot = lax.rem(turn, 2)

        def copies(turn_of, at):
            first, cols = (turn_of // 3) * AT, lax.rem(turn_of, 3) * 2
            return [
                pltpu.make_async_copy(
                    lines.at[at, half].reshape(AT, 2, 2, LANES),
                    out.at[pl.ds(first, AT), :, :, pl.ds(pl.multiple_of((cols + half) * LANES, LANES), LANES)],
                    sems.at[at, half])
                for half in range(2)
            ]

    def run(acc0, acc1):
        def left_limbs(n):
            m, u, j = steps[n]
            for top in range(0, AT, PIECE):
                for i, limb in enumerate(limbs(lefts[m][u, top:top + PIECE, j:j + BLK])):
                    bufs[n % 2][i, top:top + PIECE] = limb

        def z_limbs(n):
            m, u, j = steps[n]
            for t in range(2):
                for top in range(0, BLK, PIECE):
                    for i, limb in enumerate(limbs(zs[m][u, t, j + top:j + top + PIECE])):
                        zbufs[n % 2][i, t, top:top + PIECE] = limb

        z_limbs(0)
        left_limbs(0)
        reg = 0
        for n in range(len(steps)):
            start = reg
            for t, acc in enumerate((acc0, acc1)):
                reg = full_product(acc, t, [bufs[n % 2][i] for i in range(3)], [zbufs[n % 2][i, t] for i in range(3)], False, start)
            if n + 1 < len(steps):
                z_limbs(n + 1)
                left_limbs(n + 1)
        if final:
            @pl.when((lax.rem(col, 2) == 0) & (turn >= 2))
            def _():
                for copy in copies(turn - 2, slot):
                    copy.wait()

        for t, acc in enumerate((acc0, acc1)):
            got = pltpu.matmul_pop(acc)
            if has_prev:
                got = got + prev[:, t * BLK:(t + 1) * BLK]
            if final:
                for half in range(2):
                    lines[slot, half, pl.ds(2 * lax.rem(col, 2) + t, AT, stride=4), :] = got[:, half * LANES:(half + 1) * LANES]
            else:
                out[:, t * BLK:(t + 1) * BLK] = got

    pl.run_scoped(run, pltpu.ACC(0)((AT, BLK), F32), pltpu.ACC(1)((AT, BLK), F32))

    if final:
        turns = pl.num_programs(0) * 3

        @pl.when(lax.rem(col, 2) == 1)
        def _():
            for copy in copies(turn, slot):
                copy.start()

        @pl.when((lax.rem(col, 2) == 1) & (turn == turns - 1))
        def _():
            for copy in copies(turn - 1, 1 - slot) + copies(turn, slot):
                copy.wait()


def params():
    return pltpu.CompilerParams(vmem_limit_bytes=VMEM_LIMIT)


def cost(flops, nbytes):
    return pl.CostEstimate(flops=flops, bytes_accessed=nbytes, transcendentals=0)


CHUNKS = ((0, 256), (256, 256), (512, 256), (768, 256), (1024, 512))


def solution(mesh):
    def local_apply(wave_blk, left_rows, mpo_ten, right_rows):
        rows_c, cols_f = wave_blk.shape[0], wave_blk.shape[3]
        by, bx = lax.axis_index('by'), lax.axis_index('bx')
        left = left_rows.transpose(1, 0, 2)
        right = right_rows.transpose(1, 0, 2)
        mpo_flat = mpo_ten.reshape(-1)
        own = by.astype(jnp.int32)[None]

        def to_lines(chunks):
            base = chunks[0][0]
            bounds = [((lo - base) // LINE_CT, (lo + n - base) // LINE_CT) for lo, n in chunks]
            return pl.pallas_call(
                lambda *refs: to_lines_kernel(base, bounds, *refs),
                grid=(bounds[-1][1],),
                in_specs=[pl.BlockSpec(memory_space=pl.ANY)],
                out_specs=[pl.BlockSpec((6, LINE_CT * 4, LANES), lambda i, lo=lo, hi=hi: (0, jnp.clip(i - lo, 0, hi - lo - 1), 0)) for lo, hi in bounds],
                out_shape=[jax.ShapeDtypeStruct((6, n * 4, LANES), F32) for _, n in chunks],
                scratch_shapes=[pltpu.SemaphoreType.DMA((6,))],
                compiler_params=params(),
                cost_estimate=cost(10**9 * bounds[-1][1], bounds[-1][1] * 4 * 2**20),
                name='to_lines',
            )(wave_blk)

        lines = to_lines(CHUNKS[:1]) + to_lines(CHUNKS[1:])
        gathered = [lax.all_gather(line, 'by', axis=0, tiled=False) for line in lines]

        part = pl.pallas_call(
            lambda idx, *refs: local_kernel(rows_c // CT, *refs),
            grid_spec=pltpu.PrefetchScalarGridSpec(
                num_scalar_prefetch=1,
                grid=(rows_c // CT,),
                in_specs=[
                    pl.BlockSpec(memory_space=pl.ANY),
                    pl.BlockSpec((3, 768, 768), lambda i, idx: (0, 0, idx[0]), pipeline_mode=pl.Buffered(1)),
                ],
                out_specs=pl.BlockSpec((12, CT, 768), lambda i, idx: (0, i, 0)),
                scratch_shapes=[pltpu.VMEM((2, 6, CT * 4, LANES), F32), pltpu.SemaphoreType.DMA((2, 6))]
                + [pltpu.VMEM((3, 2, 2 * CT, BLK), BF16)] * 3,
            ),
            out_shape=jax.ShapeDtypeStruct((12, rows_c, 768), F32),
            compiler_params=params(),
            cost_estimate=cost(2 * rows_c * 4 * 768 * 2304 * 6, 120 * 2**20),
            name='local_part',
        )(own, wave_blk, right)

        def first(k, got):
            lo, n = CHUNKS[k]
            tiles = n // CT
            return pl.pallas_call(
                remote_kernel,
                grid_spec=pltpu.PrefetchScalarGridSpec(
                    num_scalar_prefetch=1,
                    grid=(tiles * 3,),
                    in_specs=[
                        pl.BlockSpec(memory_space=pltpu.SMEM),
                        pl.BlockSpec((4, 6, CT * 4, LANES), lambda i, idx: (0, 0, i // 3, 0)),
                        pl.BlockSpec((3, BLK, 3072), lambda i, idx: (0, i % 3, 0)),
                        pl.BlockSpec((12, CT, BLK), lambda i, idx: (0, lo // CT + i // 3, i % 3)),
                    ],
                    out_specs=pl.BlockSpec((3, 4, CT, BLK), lambda i, idx: (0, 0, i // 3, i % 3)),
                    scratch_shapes=[pltpu.VMEM((9, 3, 2, 2 * CT, BLK), BF16), pltpu.VMEM((12, CT, BLK), F32)],
                ),
                out_shape=jax.ShapeDtypeStruct((3, 4, n, 768), F32),
                compiler_params=params(),
                cost_estimate=cost(2 * n * 4 * 2304 * 2304 * 6, 60 * 2**20),
                name='remote_part',
            )(own, mpo_flat, got, right, part)

        def second(group, mine, theirs, prev, final):
            width = CHUNKS[group[0]][1]
            srcs = [(bx, k) for k in group] + [(1 - bx, k) for k in group]
            where = jnp.stack([(b * rows_c + CHUNKS[k][0]) // width for b, k in srcs]).astype(jnp.int32)
            n_src = len(srcs)
            in_specs = [pl.BlockSpec((3, AT, width), lambda a, n, idx, m=m: (0, a, idx[m])) for m in range(n_src)]
            in_specs += [pl.BlockSpec((3, 2, width, BLK), lambda a, n, idx: (0, n % 2, 0, n // 2))] * n_src
            operands = [left] * n_src + mine + theirs
            if prev is not None:
                in_specs.append(pl.BlockSpec((AT, 2 * BLK), lambda a, n, idx: (a, n)))
                operands.append(prev)
            scratch = [pltpu.VMEM((3, AT, BLK), BF16)] * 2 + [pltpu.VMEM((3, 2, BLK, BLK), BF16)] * 2
            if final:
                out_spec = pl.BlockSpec(memory_space=pl.ANY)
                out_shape = jax.ShapeDtypeStruct((rows_c, 2, 2, cols_f), F32)
                scratch += [pltpu.VMEM((2, 2, AT * 4, LANES), F32), pltpu.SemaphoreType.DMA((2, 2))]
            else:
                out_spec = pl.BlockSpec((AT, 2 * BLK), lambda a, n, idx: (a, n))
                out_shape = jax.ShapeDtypeStruct((rows_c, 3072), F32)
            return pl.pallas_call(
                lambda idx, *refs: second_kernel(n_src, width, prev is not None, final, *refs),
                grid_spec=pltpu.PrefetchScalarGridSpec(
                    num_scalar_prefetch=1,
                    grid=(rows_c // AT, 6),
                    in_specs=in_specs,
                    out_specs=out_spec,
                    scratch_shapes=scratch,
                ),
                out_shape=out_shape,
                compiler_params=params(),
                cost_estimate=cost(2 * rows_c * 3072 * 3 * width * n_src * 6, 100 * 2**20),
                name='second_part',
            )(where, *operands)

        mine, theirs = [], []

        def stage(k):
            z = first(k, gathered[k])
            mine.append(z)
            theirs.append(lax.ppermute(z, 'bx', [(0, 1), (1, 0)]))

        def apply(group, prev, final):
            return second(group, [mine[k] for k in group], [theirs[k] for k in group], prev, final)

        def after(k, val):
            gathered[k], val = lax.optimization_barrier((gathered[k], val))
            return val

        stage(0)
        stage(1)
        acc = apply([0], None, False)
        acc = after(2, acc)
        stage(2)
        stage(3)
        acc = apply([1, 2], acc, False)
        acc = after(4, acc)
        stage(4)
        acc, mine[4] = lax.optimization_barrier((acc, mine[4]))
        acc = apply([3], acc, False)
        return apply([4], acc, True)

    return jax.shard_map(local_apply, mesh=mesh, in_specs=(P('bx', None, None, 'by'), P('bx', None, None), P(), P('by', None, None)), out_specs=P('bx', None, None, 'by'), check_vma=False)
```

time: 1330 us -> 1310 us (0.985)
  Pallas kernels: 1300 us -> 1260 us
  waiting for transfers between devices: 1.29 us -> 28.1 us
    pallas_call x14 -> x12, Pallas kernels: 1300 us -> 1260 us  [the longest x4 570 us: second(): pl.pallas_call(lambda idx, *refs: second_kernel(n_src, width, prev is not...]
    ppermute x6 -> x5, waiting for transfers between devices: 0.02 us -> 26.9 us  [stage(): theirs.append(lax.ppermute(z, 'bx', [(0, 1), (1, 0)]))]
  transfers between devices with their start and end apart: 12 -> 10, of which waited for: 0 -> 2; matrix products, arithmetic and copies ran while one was open for 0% -> 0% of each run, Pallas kernels for 89% -> 82%
where the time goes in v2:
time: 1310 us; the launch traced here: 1300 us
  Pallas kernels  1260 us (96%)
  waiting for transfers between devices  28.1 us (2%)
  between operations  13.7 us (1%)
    pallas_call x4, Pallas kernels, second(): pl.pallas_call(lambda idx, *refs: second_kernel(n_src, width, prev is not...  570 us
    pallas_call x5, Pallas kernels, first(): pl.pallas_call(remote_kernel, grid_spec=pltpu.PrefetchScalarGridSpec(num_...  518 us
    pallas_call x1, Pallas kernels, local_apply(): pl.pallas_call(lambda idx, *refs: local_kernel(rows_c // CT, *refs), grid...  144 us
    ppermute x5, waiting for transfers between devices, stage(): theirs.append(lax.ppermute(z, 'bx', [(0, 1), (1, 0)]))  26.9 us
  transfers between devices with their start and end apart: 10, of which 2 were waited for; matrix products, arithmetic and copies ran while one was open for 0% of the time, Pallas kernels for 82%

profile of v2, /device:TPU:0, one launch (start us, length us, event | category | flops | bytes accessed | tf_op | source)
XLA Modules:
  0.0 1303.7 jit_solution(12479239761682212400)
XLA Ops:
  6.5 4.5 to_lines.3
  11.0 0.0 all-gather.17.cloned.1.call-update
  11.0 0.0 all-gather.13.cloned.1.call-start
  11.1 19.6 %to_lines.2 = (f32[6,1024,128]{2,1,0:T(8,128)}, f32[6,1024,128]{2,1,0:T(8,128)}, f32[6,1024,128]{2,1,0:T(8,128)}, f32[6,2048,128]{2,1,0:T(8,128)}) custom-call(f32[1536,2,2,768]{3,2,1,0:T(2,128)} %refs_0_.5), custom_call_target="tpu_custom_call" | custom-call | flops 10000000000 | bytes 41943040 | tf_op jit(solution)/shard_map/to_lines/pallas_call | solution.py:290
  30.7 0.0 all-gather.13.cloned.1.call-update
  30.8 0.0 all-gather.15.cloned.1.call-start
  30.8 0.7 all-gather.15.cloned.1.call-update
  31.5 0.0 all-gather.11.cloned.1.call-start
  31.5 0.5 all-gather.11.cloned.1.call-update
  32.1 0.0 all-gather.19.cloned.1.call-start
  32.1 0.7 reshape.3.w_ref
  32.8 144.0 %local_part.1.part = f32[12,1536,768]{2,1,0:T(8,128)} custom-call(s32[1]{0:T(128)} %bitcast.8.idx.own_ref, f32[1536,2,2,768]{3,2,1,0:T(2,128)} %refs_0_.5, f32[3,768,3072]{2,1,0:T(8,128)} %bitcast.28), custom_call_target="tpu_custom_call" | custom-call | flops 130459631616 | bytes 125829120 | tf_op jit(solution)/shard_map/local_part/pallas_call | solution.py:305
  176.8 0.0 all-gather.17.cloned.1.call-done
  176.8 87.7 %remote_part.6.refs_2_ = f32[3,4,256,768]{3,2,1,0:T(8,128)} custom-call(s32[1]{0:T(128)} %bitcast.8.idx.own_ref, f32[36]{0:T(128)} %reshape.3.w_ref, f32[4,6,1024,128]{3,2,1,0:T(8,128)} %bitcast.38, f32[3,768,3072]{2,1,0:T(8,128)} %bitcast.29, f32[12,1536,768]{2,1,0:T(8,128)} %local_part.1.part), custom_call_target="tpu_custom_call" | custom-call | flops 65229815808 | bytes 62914560 | tf_op jit(solution)/shard_map/remote_part/pallas_call | solution.py:327
  264.5 0.8 collective-permute-start
  265.3 0.7 pad_add_fusion.2.idx
  266.0 87.5 %remote_part.5.refs_4_ = f32[3,4,256,768]{3,2,1,0:T(8,128)} custom-call(s32[1]{0:T(128)} %bitcast.8.idx.own_ref, f32[36]{0:T(128)} %reshape.3.w_ref, f32[4,6,1024,128]{3,2,1,0:T(8,128)} %bitcast.37, f32[3,768,3072]{2,1,0:T(8,128)} %bitcast.30, f32[12,1536,768]{2,1,0:T(8,128)} %local_part.1.part), custom_call_target="tpu_custom_call" | custom-call | flops 65229815808 | bytes 62914560 | tf_op jit(solution)/shard_map/remote_part/pallas_call | solution.py:327
  353.5 96.7 %second_part.4.refs_8_ = f32[1536,3072]{1,0:T(8,128)} custom-call(s32[2]{0:T(128)} %pad_add_fusion.2.idx, f32[3,1536,3072]{2,1,0:T(8,128)} %bitcast.18, f32[3,1536,3072]{2,1,0:T(8,128)} %bitcast.19, f32[3,4,256,768]{3,2,1,0:T(8,128)} %remote_part.6.refs_2_, f32[3,4,256,768]{3,2,1,0:T(8,128)} %collective-permute-done.refs_3_), custom_call_target="tpu_custom_call" | custom-call | flops 86973087744 | bytes 104857600 | tf_op jit(solution)/shard_map/second_part/pallas_call | solution.py:366
  450.2 87.6 %remote_part.7.refs_5_ = f32[3,4,256,768]{3,2,1,0:T(8,128)} custom-call(s32[1]{0:T(128)} %bitcast.8.idx.own_ref, f32[36]{0:T(128)} %reshape.3.w_ref, f32[4,6,1024,128]{3,2,1,0:T(8,128)} %bitcast.36, f32[3,768,3072]{2,1,0:T(8,128)} %bitcast.31, f32[12,1536,768]{2,1,0:T(8,128)} %local_part.1.part), custom_call_target="tpu_custom_call" | custom-call | flops 65229815808 | bytes 62914560 | tf_op jit(solution)/shard_map/remote_part/pallas_call | solution.py:327
  537.8 0.5 collective-permute-start.2
  538.3 0.6 pad_add_fusion.1.idx
  538.9 13.7 %collective-permute-done.2.refs_7_ = f32[3,4,256,768]{3,2,1,0:T(8,128)} collective-permute-done((f32[3,4,256,768]{3,2,1,0:T(8,128)}, f32[3,4,256,768]{3,2,1,0:T(8,128)}, u32[]{:S(2)}, u32[]{:S(2)}) %collective-permute-start.2) | collective-permute-done | bytes 9437216 | tf_op jit(solution)/shard_map/ppermute | solution.py:386
  552.6 188.3 %second_part.5.refs_4_ = f32[1536,3072]{1,0:T(8,128)} custom-call(s32[4]{0:T(128)} %pad_add_fusion.1.idx, f32[3,1536,3072]{2,1,0:T(8,128)} %bitcast.20, f32[3,1536,3072]{2,1,0:T(8,128)} %bitcast.21, f32[3,1536,3072]{2,1,0:T(8,128)} %bitcast.22, f32[3,1536,3072]{2,1,0:T(8,128)} %bitcast.23, f32[3,4,256,768]{3,2,1,0:T(8,128)} %remote_part.5.refs_4_, ...), custom_call_target="tpu_custom_call" | custom-call | flops 173946175488 | bytes 104857600 | tf_op jit(solution)/shard_map/second_part/pallas_call | solution.py:366
  740.9 168.1 %remote_part.8.refs_2_ = f32[3,4,512,768]{3,2,1,0:T(8,128)} custom-call(s32[1]{0:T(128)} %bitcast.8.idx.own_ref, f32[36]{0:T(128)} %reshape.3.w_ref, f32[4,6,2048,128]{3,2,1,0:T(8,128)} %bitcast.34, f32[3,768,3072]{2,1,0:T(8,128)} %bitcast.32, f32[12,1536,768]{2,1,0:T(8,128)} %local_part.1.part), custom_call_target="tpu_custom_call" | custom-call | flops 130459631616 | bytes 62914560 | tf_op jit(solution)/shard_map/remote_part/pallas_call | solution.py:327
  909.0 0.3 collective-permute-start.3
  909.4 87.5 %remote_part.9.refs_2_ = f32[3,4,256,768]{3,2,1,0:T(8,128)} custom-call(s32[1]{0:T(128)} %bitcast.8.idx.own_ref, f32[36]{0:T(128)} %reshape.3.w_ref, f32[4,6,1024,128]{3,2,1,0:T(8,128)} %bitcast.35, f32[3,768,3072]{2,1,0:T(8,128)} %bitcast.33, f32[12,1536,768]{2,1,0:T(8,128)} %local_part.1.part), custom_call_target="tpu_custom_call" | custom-call | flops 65229815808 | bytes 62914560 | tf_op jit(solution)/shard_map/remote_part/pallas_call | solution.py:327
  996.8 0.2 collective-permute-start.4
  997.0 0.6 pad_add_fusion.3.idx
  997.6 0.7 pad_add_fusion.idx
  998.2 13.2 %collective-permute-done.4.refs_3_ = f32[3,4,256,768]{3,2,1,0:T(8,128)} collective-permute-done((f32[3,4,256,768]{3,2,1,0:T(8,128)}, f32[3,4,256,768]{3,2,1,0:T(8,128)}, u32[]{:S(2)}, u32[]{:S(2)}) %collective-permute-start.4) | collective-permute-done | bytes 9437216 | tf_op jit(solution)/shard_map/ppermute | solution.py:386
  1011.4 96.9 %second_part.6.refs_4_ = f32[1536,3072]{1,0:T(8,128)} custom-call(s32[2]{0:T(128)} %pad_add_fusion.3.idx, f32[3,1536,3072]{2,1,0:T(8,128)} %bitcast.24, f32[3,1536,3072]{2,1,0:T(8,128)} %bitcast.25, f32[3,4,256,768]{3,2,1,0:T(8,128)} %remote_part.9.refs_2_, f32[3,4,256,768]{3,2,1,0:T(8,128)} %collective-permute-done.4.refs_3_, f32[1536,3072]{1,0:T(8,128)} %second_part.5.refs_4_), custom_call_target="tpu_custom_call" | custom-call | flops 86973087744 | bytes 104857600 | tf_op jit(solution)/shard_map/second_part/pallas_call | solution.py:366
  1108.3 188.4 %second_part.7 = f32[1536,2,2,768]{3,2,1,0:T(2,128)} custom-call(s32[2]{0:T(128)} %pad_add_fusion.idx, f32[3,1536,3072]{2,1,0:T(8,128)} %bitcast.26, f32[3,1536,3072]{2,1,0:T(8,128)} %bitcast.27, f32[3,4,512,768]{3,2,1,0:T(8,128)} %remote_part.8.refs_2_, f32[3,4,512,768]{3,2,1,0:T(8,128)} %collective-permute-done.3.refs_3_, f32[1536,3072]{1,0:T(8,128)} %second_part.6.refs_4_), custom_call_target="tpu_custom_call" | custom-call | flops 173946175488 | bytes 104857600 | tf_op jit(solution)/shard_map/second_part/pallas_call | solution.py:366
  (12 shorter events, 0.0 us)
Async XLA Ops:
  6.5 170.3 %all-gather.17.cloned.1.call-start = ((), (), s32[]{:S(2)}) async-start(), calls=%async_computation.3 | async-start | bytes 15728640 | tf_op jit(solution)/shard_map/all_gather | solution.py:303
  11.0 254.9 %all-gather.13.cloned.1.call-start = ((), (), s32[]{:S(2)}) async-start(), calls=%async_computation.1 | async-start | bytes 15728640 | tf_op jit(solution)/shard_map/all_gather | solution.py:303
  30.7 1.4 copy-start
  30.8 419.4 %all-gather.15.cloned.1.call-start = ((), (), s32[]{:S(2)}) async-start(), calls=%async_computation.2 | async-start | bytes 15728640 | tf_op jit(solution)/shard_map/all_gather | solution.py:303
  31.5 709.4 %all-gather.11.cloned.1.call-start = ((), (), s32[]{:S(2)}) async-start(), calls=%async_computation | async-start | bytes 31457280 | tf_op jit(solution)/shard_map/all_gather | solution.py:303
  32.1 877.3 %all-gather.19.cloned.1.call-start = ((), (), s32[]{:S(2)}) async-start(), calls=%async_computation.4 | async-start | bytes 15728640 | tf_op jit(solution)/shard_map/all_gather | solution.py:303
  264.5 89.0 %collective-permute-start = (f32[3,4,256,768]{3,2,1,0:T(8,128)}, f32[3,4,256,768]{3,2,1,0:T(8,128)}, u32[]{:S(2)}, u32[]{:S(2)}) collective-permute-start(f32[3,4,256,768]{3,2,1,0:T(8,128)} %remote_part.6.refs_2_), channel_id=1, source_target_pairs={{0,1},{1,0},{2,3},{3,2},{4,5},{5,4},{6,7},{7,6}} | collective-permute-start | bytes 28311560 | tf_op jit(solution)/shard_map/ppermute | solution.py:386
  353.5 185.5 %collective-permute-start.1 = (f32[3,4,256,768]{3,2,1,0:T(8,128)}, f32[3,4,256,768]{3,2,1,0:T(8,128)}, u32[]{:S(2)}, u32[]{:S(2)}) collective-permute-start(f32[3,4,256,768]{3,2,1,0:T(8,128)} %remote_part.5.refs_4_), channel_id=1, source_target_pairs={{0,1},{1,0},{2,3},{3,2},{4,5},{5,4},{6,7},{7,6}} | collective-permute-start | bytes 28311560 | tf_op jit(solution)/shard_map/ppermute | solution.py:386
  537.8 14.8 %collective-permute-start.2 = (f32[3,4,256,768]{3,2,1,0:T(8,128)}, f32[3,4,256,768]{3,2,1,0:T(8,128)}, u32[]{:S(2)}, u32[]{:S(2)}) collective-permute-start(f32[3,4,256,768]{3,2,1,0:T(8,128)} %remote_part.7.refs_5_), channel_id=1, source_target_pairs={{0,1},{1,0},{2,3},{3,2},{4,5},{5,4},{6,7},{7,6}} | collective-permute-start | bytes 28311560 | tf_op jit(solution)/shard_map/ppermute | solution.py:386
  909.0 199.3 %collective-permute-start.3 = (f32[3,4,512,768]{3,2,1,0:T(8,128)}, f32[3,4,512,768]{3,2,1,0:T(8,128)}, u32[]{:S(2)}, u32[]{:S(2)}) collective-permute-start(f32[3,4,512,768]{3,2,1,0:T(8,128)} %remote_part.8.refs_2_), channel_id=1, source_target_pairs={{0,1},{1,0},{2,3},{3,2},{4,5},{5,4},{6,7},{7,6}} | collective-permute-start | bytes 56623112 | tf_op jit(solution)/shard_map/ppermute | solution.py:386
  996.8 14.6 %collective-permute-start.4 = (f32[3,4,256,768]{3,2,1,0:T(8,128)}, f32[3,4,256,768]{3,2,1,0:T(8,128)}, u32[]{:S(2)}, u32[]{:S(2)}) collective-permute-start(f32[3,4,256,768]{3,2,1,0:T(8,128)} %remote_part.9.refs_2_), channel_id=1, source_target_pairs={{0,1},{1,0},{2,3},{3,2},{4,5},{5,4},{6,7},{7,6}} | collective-permute-start | bytes 28311560 | tf_op jit(solution)/shard_map/ppermute | solution.py:386
Sparse Core Ops, SparseCore 0:
  11.2 119.6 all-gather.16
  132.6 116.8 all-gather.12
  251.3 116.8 all-gather.14
  369.8 222.1 all-gather.10
  593.6 116.8 all-gather.18

commit v3 on v2

--- a/solution.py
+++ b/solution.py
@@ -388,20 +388,28 @@
         def apply(group, prev, final):
             return second(group, [mine[k] for k in group], [theirs[k] for k in group], prev, final)
 
-        def after(k, val):
+        def before(k, val):
             gathered[k], val = lax.optimization_barrier((gathered[k], val))
             return val
 
+        def behind(k, val):
+            val, mine[k] = lax.optimization_barrier((val, mine[k]))
+            return val
+
         stage(0)
         stage(1)
+        mine[0] = behind(1, mine[0])
         acc = apply([0], None, False)
-        acc = after(2, acc)
+        acc = before(2, acc)
         stage(2)
+        mine[2] = before(3, mine[2])
         stage(3)
+        acc = behind(3, acc)
         acc = apply([1, 2], acc, False)
-        acc = after(4, acc)
+        acc = before(4, acc)
+        gathered[4], theirs[3] = lax.optimization_barrier((gathered[4], theirs[3]))
         stage(4)
-        acc, mine[4] = lax.optimization_barrier((acc, mine[4]))
+        acc = behind(4, acc)
         acc = apply([3], acc, False)
         return apply([4], acc, True)
 

time: 1310 us -> 1280 us (0.977)
  waiting for transfers between devices: 28.1 us -> 1.29 us
    ppermute x5, waiting for transfers between devices: 26.9 us -> 0.01 us  [stage(): theirs.append(lax.ppermute(z, 'bx', [(0, 1), (1, 0)]))]
  transfers between devices with their start and end apart: 10 -> 10, of which waited for: 2 -> 0; matrix products, arithmetic and copies ran while one was open for 0% -> 0% of each run, Pallas kernels for 82% -> 70%
where the time goes in v3:
time: 1280 us
  Pallas kernels  1260 us (98%)
  between operations  13.7 us (1%)
    pallas_call x4, Pallas kernels, second(): pl.pallas_call(lambda idx, *refs: second_kernel(n_src, width, prev is not...  570 us
    pallas_call x5, Pallas kernels, first(): pl.pallas_call(remote_kernel, grid_spec=pltpu.PrefetchScalarGridSpec(num_...  518 us
    pallas_call x1, Pallas kernels, local_apply(): pl.pallas_call(lambda idx, *refs: local_kernel(rows_c // CT, *refs), grid...  144 us
  transfers between devices with their start and end apart: 10, of which 0 were waited for; matrix products, arithmetic and copies ran while one was open for 0% of the time, Pallas kernels for 70%

profile of v3, /device:TPU:0, one launch (start us, length us, event | category | flops | bytes accessed | tf_op | source)
XLA Modules:
  0.0 1276.6 jit_solution(15715045465850637072)
XLA Ops:
  6.5 4.5 to_lines.3
  11.0 0.0 all-gather.13.cloned.1.call-update
  11.1 0.0 all-gather.15.cloned.1.call-start
  11.1 19.6 %to_lines.2 = (f32[6,1024,128]{2,1,0:T(8,128)}, f32[6,1024,128]{2,1,0:T(8,128)}, f32[6,1024,128]{2,1,0:T(8,128)}, f32[6,2048,128]{2,1,0:T(8,128)}) custom-call(f32[1536,2,2,768]{3,2,1,0:T(2,128)} %refs_0_.5), custom_call_target="tpu_custom_call" | custom-call | flops 10000000000 | bytes 41943040 | tf_op jit(solution)/shard_map/to_lines/pallas_call | solution.py:290
  30.7 0.0 all-gather.15.cloned.1.call-update
  30.7 0.0 all-gather.19.cloned.1.call-start
  30.8 0.7 all-gather.19.cloned.1.call-update
  31.5 0.0 all-gather.17.cloned.1.call-start
  31.5 0.5 all-gather.17.cloned.1.call-update
  32.0 0.0 all-gather.11.cloned.1.call-start
  32.1 0.6 reshape.3.w_ref
  32.7 143.9 %local_part.1.part = f32[12,1536,768]{2,1,0:T(8,128)} custom-call(s32[1]{0:T(128)} %bitcast.8.idx.own_ref, f32[1536,2,2,768]{3,2,1,0:T(2,128)} %refs_0_.5, f32[3,768,3072]{2,1,0:T(8,128)} %bitcast.28), custom_call_target="tpu_custom_call" | custom-call | flops 130459631616 | bytes 125829120 | tf_op jit(solution)/shard_map/local_part/pallas_call | solution.py:305
  176.7 0.0 all-gather.13.cloned.1.call-done
  176.7 87.7 %remote_part.5.refs_2_ = f32[3,4,256,768]{3,2,1,0:T(8,128)} custom-call(s32[1]{0:T(128)} %bitcast.8.idx.own_ref, f32[36]{0:T(128)} %reshape.3.w_ref, f32[4,6,1024,128]{3,2,1,0:T(8,128)} %bitcast.38, f32[3,768,3072]{2,1,0:T(8,128)} %bitcast.29, f32[12,1536,768]{2,1,0:T(8,128)} %local_part.1.part), custom_call_target="tpu_custom_call" | custom-call | flops 65229815808 | bytes 62914560 | tf_op jit(solution)/shard_map/remote_part/pallas_call | solution.py:327
  264.4 0.9 collective-permute-start
  265.3 0.0 all-gather.11.cloned.1.call-update
  265.4 0.7 pad_add_fusion.2.idx
  266.0 87.4 %remote_part.6.refs_4_ = f32[3,4,256,768]{3,2,1,0:T(8,128)} custom-call(s32[1]{0:T(128)} %bitcast.8.idx.own_ref, f32[36]{0:T(128)} %reshape.3.w_ref, f32[4,6,1024,128]{3,2,1,0:T(8,128)} %bitcast.37, f32[3,768,3072]{2,1,0:T(8,128)} %bitcast.30, f32[12,1536,768]{2,1,0:T(8,128)} %local_part.1.part), custom_call_target="tpu_custom_call" | custom-call | flops 65229815808 | bytes 62914560 | tf_op jit(solution)/shard_map/remote_part/pallas_call | solution.py:327
  353.4 0.0 collective-permute-start.1
  353.5 96.7 %second_part.4.refs_8_ = f32[1536,3072]{1,0:T(8,128)} custom-call(s32[2]{0:T(128)} %pad_add_fusion.2.idx, f32[3,1536,3072]{2,1,0:T(8,128)} %bitcast.18, f32[3,1536,3072]{2,1,0:T(8,128)} %bitcast.19, f32[3,4,256,768]{3,2,1,0:T(8,128)} %remote_part.5.refs_2_, f32[3,4,256,768]{3,2,1,0:T(8,128)} %collective-permute-done.refs_3_), custom_call_target="tpu_custom_call" | custom-call | flops 86973087744 | bytes 104857600 | tf_op jit(solution)/shard_map/second_part/pallas_call | solution.py:366
  450.1 87.5 %remote_part.7.refs_5_ = f32[3,4,256,768]{3,2,1,0:T(8,128)} custom-call(s32[1]{0:T(128)} %bitcast.8.idx.own_ref, f32[36]{0:T(128)} %reshape.3.w_ref, f32[4,6,1024,128]{3,2,1,0:T(8,128)} %bitcast.36, f32[3,768,3072]{2,1,0:T(8,128)} %bitcast.31, f32[12,1536,768]{2,1,0:T(8,128)} %local_part.1.part), custom_call_target="tpu_custom_call" | custom-call | flops 65229815808 | bytes 62914560 | tf_op jit(solution)/shard_map/remote_part/pallas_call | solution.py:327
  537.6 0.5 collective-permute-start.2
  538.1 0.7 pad_add_fusion.1.idx
  538.8 87.5 %remote_part.8.refs_2_ = f32[3,4,256,768]{3,2,1,0:T(8,128)} custom-call(s32[1]{0:T(128)} %bitcast.8.idx.own_ref, f32[36]{0:T(128)} %reshape.3.w_ref, f32[4,6,1024,128]{3,2,1,0:T(8,128)} %bitcast.35, f32[3,768,3072]{2,1,0:T(8,128)} %bitcast.32, f32[12,1536,768]{2,1,0:T(8,128)} %local_part.1.part), custom_call_target="tpu_custom_call" | custom-call | flops 65229815808 | bytes 62914560 | tf_op jit(solution)/shard_map/remote_part/pallas_call | solution.py:327
  626.2 0.0 collective-permute-start.3
  626.3 188.3 %second_part.5.refs_4_ = f32[1536,3072]{1,0:T(8,128)} custom-call(s32[4]{0:T(128)} %pad_add_fusion.1.idx, f32[3,1536,3072]{2,1,0:T(8,128)} %bitcast.20, f32[3,1536,3072]{2,1,0:T(8,128)} %bitcast.21, f32[3,1536,3072]{2,1,0:T(8,128)} %bitcast.22, f32[3,1536,3072]{2,1,0:T(8,128)} %bitcast.23, f32[3,4,256,768]{3,2,1,0:T(8,128)} %remote_part.6.refs_4_, ...), custom_call_target="tpu_custom_call" | custom-call | flops 173946175488 | bytes 104857600 | tf_op jit(solution)/shard_map/second_part/pallas_call | solution.py:366
  814.6 168.2 %remote_part.9.refs_2_ = f32[3,4,512,768]{3,2,1,0:T(8,128)} custom-call(s32[1]{0:T(128)} %bitcast.8.idx.own_ref, f32[36]{0:T(128)} %reshape.3.w_ref, f32[4,6,2048,128]{3,2,1,0:T(8,128)} %bitcast.34, f32[3,768,3072]{2,1,0:T(8,128)} %bitcast.33, f32[12,1536,768]{2,1,0:T(8,128)} %local_part.1.part), custom_call_target="tpu_custom_call" | custom-call | flops 130459631616 | bytes 62914560 | tf_op jit(solution)/shard_map/remote_part/pallas_call | solution.py:327
  982.8 0.5 collective-permute-start.4
  983.3 0.6 pad_add_fusion.3.idx
  983.9 0.6 pad_add_fusion.idx
  984.5 96.9 %second_part.6.refs_4_ = f32[1536,3072]{1,0:T(8,128)} custom-call(s32[2]{0:T(128)} %pad_add_fusion.3.idx, f32[3,1536,3072]{2,1,0:T(8,128)} %bitcast.24, f32[3,1536,3072]{2,1,0:T(8,128)} %bitcast.25, f32[3,4,256,768]{3,2,1,0:T(8,128)} %remote_part.8.refs_2_, f32[3,4,256,768]{3,2,1,0:T(8,128)} %collective-permute-done.3.refs_3_, f32[1536,3072]{1,0:T(8,128)} %second_part.5.refs_4_), custom_call_target="tpu_custom_call" | custom-call | flops 86973087744 | bytes 104857600 | tf_op jit(solution)/shard_map/second_part/pallas_call | solution.py:366
  1081.4 188.3 %second_part.7 = f32[1536,2,2,768]{3,2,1,0:T(2,128)} custom-call(s32[2]{0:T(128)} %pad_add_fusion.idx, f32[3,1536,3072]{2,1,0:T(8,128)} %bitcast.26, f32[3,1536,3072]{2,1,0:T(8,128)} %bitcast.27, f32[3,4,512,768]{3,2,1,0:T(8,128)} %remote_part.9.refs_2_, f32[3,4,512,768]{3,2,1,0:T(8,128)} %collective-permute-done.4.refs_3_, f32[1536,3072]{1,0:T(8,128)} %second_part.6.refs_4_), custom_call_target="tpu_custom_call" | custom-call | flops 173946175488 | bytes 104857600 | tf_op jit(solution)/shard_map/second_part/pallas_call | solution.py:366
  (12 shorter events, 0.0 us)
Async XLA Ops:
  6.5 170.2 %all-gather.13.cloned.1.call-start = ((), (), s32[]{:S(2)}) async-start(), calls=%async_computation.1 | async-start | bytes 15728640 | tf_op jit(solution)/shard_map/all_gather | solution.py:303
  11.0 21.1 %copy-start = (f32[3,2,2,3]{3,2,1,0:T(2,128)S(1)}, f32[3,2,2,3]{3,2,1,0:T(2,128)}, u32[]{:S(2)}) copy-start(f32[3,2,2,3]{3,2,1,0:T(2,128)} %param.6) | copy-start | bytes 436
  11.1 255.0 %all-gather.15.cloned.1.call-start = ((), (), s32[]{:S(2)}) async-start(), calls=%async_computation.2 | async-start | bytes 15728640 | tf_op jit(solution)/shard_map/all_gather | solution.py:303
  30.7 419.4 %all-gather.19.cloned.1.call-start = ((), (), s32[]{:S(2)}) async-start(), calls=%async_computation.4 | async-start | bytes 15728640 | tf_op jit(solution)/shard_map/all_gather | solution.py:303
  31.5 507.3 %all-gather.17.cloned.1.call-start = ((), (), s32[]{:S(2)}) async-start(), calls=%async_computation.3 | async-start | bytes 15728640 | tf_op jit(solution)/shard_map/all_gather | solution.py:303
  32.0 782.5 %all-gather.11.cloned.1.call-start = ((), (), s32[]{:S(2)}) async-start(), calls=%async_computation | async-start | bytes 31457280 | tf_op jit(solution)/shard_map/all_gather | solution.py:303
  264.4 89.0 %collective-permute-start = (f32[3,4,256,768]{3,2,1,0:T(8,128)}, f32[3,4,256,768]{3,2,1,0:T(8,128)}, u32[]{:S(2)}, u32[]{:S(2)}) collective-permute-start(f32[3,4,256,768]{3,2,1,0:T(8,128)} %remote_part.5.refs_2_), channel_id=1, source_target_pairs={{0,1},{1,0},{2,3},{3,2},{4,5},{5,4},{6,7},{7,6}} | collective-permute-start | bytes 28311560 | tf_op jit(solution)/shard_map/ppermute | solution.py:386
  353.4 272.9 %collective-permute-start.1 = (f32[3,4,256,768]{3,2,1,0:T(8,128)}, f32[3,4,256,768]{3,2,1,0:T(8,128)}, u32[]{:S(2)}, u32[]{:S(2)}) collective-permute-start(f32[3,4,256,768]{3,2,1,0:T(8,128)} %remote_part.6.refs_4_), channel_id=1, source_target_pairs={{0,1},{1,0},{2,3},{3,2},{4,5},{5,4},{6,7},{7,6}} | collective-permute-start | bytes 28311560 | tf_op jit(solution)/shard_map/ppermute | solution.py:386
  537.6 88.7 %collective-permute-start.2 = (f32[3,4,256,768]{3,2,1,0:T(8,128)}, f32[3,4,256,768]{3,2,1,0:T(8,128)}, u32[]{:S(2)}, u32[]{:S(2)}) collective-permute-start(f32[3,4,256,768]{3,2,1,0:T(8,128)} %remote_part.7.refs_5_), channel_id=1, source_target_pairs={{0,1},{1,0},{2,3},{3,2},{4,5},{5,4},{6,7},{7,6}} | collective-permute-start | bytes 28311560 | tf_op jit(solution)/shard_map/ppermute | solution.py:386
  626.2 188.3 %collective-permute-start.3 = (f32[3,4,256,768]{3,2,1,0:T(8,128)}, f32[3,4,256,768]{3,2,1,0:T(8,128)}, u32[]{:S(2)}, u32[]{:S(2)}) collective-permute-start(f32[3,4,256,768]{3,2,1,0:T(8,128)} %remote_part.8.refs_2_), channel_id=1, source_target_pairs={{0,1},{1,0},{2,3},{3,2},{4,5},{5,4},{6,7},{7,6}} | collective-permute-start | bytes 28311560 | tf_op jit(solution)/shard_map/ppermute | solution.py:386
  982.8 98.6 %collective-permute-start.4 = (f32[3,4,512,768]{3,2,1,0:T(8,128)}, f32[3,4,512,768]{3,2,1,0:T(8,128)}, u32[]{:S(2)}, u32[]{:S(2)}) collective-permute-start(f32[3,4,512,768]{3,2,1,0:T(8,128)} %remote_part.9.refs_2_), channel_id=1, source_target_pairs={{0,1},{1,0},{2,3},{3,2},{4,5},{5,4},{6,7},{7,6}} | collective-permute-start | bytes 56623112 | tf_op jit(solution)/shard_map/ppermute | solution.py:386
Sparse Core Ops, SparseCore 0:
  11.2 119.6 all-gather.12
  132.6 116.8 all-gather.14
  251.3 116.8 all-gather.18
  369.8 116.8 all-gather.16
  488.3 222.1 all-gather.10
